TPU v7x, 32 devices: a whole 2x2x4 slice. The times are simulated.
32 devices in a mesh: grp: 2 (over x), leaf: 16 (over z, y, core).
Axes of the slice: x: 2, y: 2, z: 4, core: 2. Of those that a mesh axis runs over, the one named last changes fastest.
Arguments:
- points: float32 [8, 32768], P(None, ('grp', 'leaf')), may hold values from -6 to 6
- rhs: float32 [16, 32768], P(None, ('grp', 'leaf')), may hold values from -6 to 6
- basis: float32 [32768, 128], P(('grp', 'leaf')), may hold values from -0.1875 to 0.1875
- transfer: float32 [32, 128, 128], P(('grp', 'leaf')), may hold values from -0.5 to 0.5
- noise: float32 [32768], P(('grp', 'leaf')), may hold values from 0.5 to 2
- inv_scale: float32 [8], replicated, may hold values from 0.15 to 0.6
- links: int32 [32, 2], P(('grp', 'leaf')), may hold values from 0 to 1, as said below
- leaf_skel: int32 [32, 128], P(('grp', 'leaf')), may hold values from 0 to 1023, as said below
- group_skel: int32 [2, 128], P('grp'), may hold values from 0 to 2047, as said below
Outputs:
- solution: float32 [16, 32768], P(None, ('grp', 'leaf'))
- residual: float32 [16, 32768], P(None, ('grp', 'leaf'))
Inputs may be any that keep to these rules, and one draw needn't show every extreme that they name: `links`: column 1 of box l equals column 0 of box l + 1; column 0 is 0 for the first box of each group of 16 and column 1 for the last. `leaf_skel`: the 128 indices of a box are distinct. `group_skel`: the 128 indices of a group are distinct.
All inputs are finite; a program needn't handle non-finite values.
Results may differ from a plain program's by a relative error of at most 0.0003.
Values sent between devices are 32-bit elements; how exact they have to be, the bound alone decides.
No kernel may reach another device: no remote copies, remote signals or barrier semaphores. Data moves between devices by JAX's collectives and lax.ppermute only.
A program may use at most 128 MiB of HBM per device.

v0:
```python
import jax
import jax.numpy as jnp
from jax import lax
from jax.sharding import PartitionSpec as P

ITERS = 2


def padded_2(value, sides, width):
    for axis, dim in sides:
        size, length = (lax.axis_size(axis), value.shape[dim])
        up = [(i, (i + 1) % size) for i in range(size - 1)]
        down = [(j, i) for i, j in up]
        last = lax.slice_in_dim(value, length - width, length, axis=dim)
        initial = lax.slice_in_dim(value, 0, width, axis=dim)
        before = lax.ppermute(last, axis, up)
        after = lax.ppermute(initial, axis, down)
        value = jnp.concatenate([before, value, after], axis=dim)
    return value


def kernel_block(left, right, inv_scale):
    first = left * inv_scale[:, None]
    second = right * inv_scale[:, None]
    cross = lax.dot_general(
        first, second, (((0,), (0,)), ((), ())), precision=lax.Precision.HIGHEST
    )
    dist = (
        jnp.sum(first * first, axis=0)[:, None]
        + jnp.sum(second * second, axis=0)[None, :]
        - 2.0 * cross
    )
    scaled = jnp.sqrt(5.0 * jnp.maximum(dist, 0.0))
    return (1.0 + scaled + scaled * scaled / 3.0) * jnp.exp(-scaled)


def contract(first, second):
    return lax.dot_general(first, second, (((1,), (1,)), ((), ())), precision=lax.Precision.HIGHEST)


def product(first, second):
    return jnp.dot(first, second, precision=lax.Precision.HIGHEST)


def two_products(residual, image):
    return lax.psum(
        (jnp.sum(residual * residual, axis=1), jnp.sum(residual * image, axis=1)), ("grp", "leaf")
    )


def local(points, rhs, basis, transfer, noise, inv_scale, links, leaf_skel, group_skel):
    width = points.shape[1]
    left_bit = links[0, 0]
    right_bit = links[0, 1]
    weight_self = 1.0 + (left_bit + right_bit).astype(jnp.float32)
    skel_pts = points[:, leaf_skel[0]]
    group_pts = lax.all_gather(skel_pts, "leaf", axis=1, tiled=True)
    top_pts = group_pts[:, group_skel[0]]
    top_all = lax.all_gather(top_pts, "grp", axis=1, tiled=True)
    kernel_top = kernel_block(top_pts, top_all, inv_scale)
    kernel_far = kernel_block(skel_pts, group_pts, inv_scale)
    kernel_self = kernel_block(points, points, inv_scale)
    square_zero = jnp.zeros((width, width), jnp.float32)
    lift = transfer[0]
    beside_all = padded_2(points, (("leaf", 1),), width)
    kernel_left = lax.cond(
        left_bit > 0,
        lambda: kernel_block(beside_all[:, :width], points, inv_scale),
        lambda: square_zero,
    )
    kernel_right = lax.cond(
        right_bit > 0,
        lambda: kernel_block(beside_all[:, 2 * width :], points, inv_scale),
        lambda: square_zero,
    )

    def near_part(vec):
        padded = padded_2(vec, (("leaf", 1),), width)
        result = weight_self * product(vec, kernel_self)
        result = result + product(padded[:, :width], kernel_left)
        return result + product(padded[:, 2 * width :], kernel_right)

    def apply(vec):
        coeff = product(vec, basis)
        far = contract(lax.all_gather(coeff, "leaf", axis=1, tiled=True), kernel_far)
        group_coeff = lax.psum(product(coeff, lift), "leaf")
        top_coeff = lax.all_gather(group_coeff, "grp", axis=1, tiled=True)
        top = contract(top_coeff, kernel_top)
        row = far + contract(top, lift)
        return noise[None, :] * vec + near_part(vec) + contract(row, basis)

    solution = jnp.zeros_like(rhs)
    residual = rhs
    image = apply(residual)
    norm_now, curve = two_products(residual, image)
    alpha = norm_now / curve
    direction, along = (residual, image)
    for step in range(ITERS):
        solution = solution + alpha[:, None] * direction
        residual = residual - alpha[:, None] * along
        if step + 1 < ITERS:
            image = apply(residual)
            norm_next, curve = two_products(residual, image)
            ratio = norm_next / norm_now
            alpha = norm_next / (curve - ratio * norm_next / alpha)
            direction = residual + ratio[:, None] * direction
            along = image + ratio[:, None] * along
            norm_now = norm_next
    return (solution, residual)


def solution(mesh):
    return jax.shard_map(
        local,
        mesh=mesh,
        in_specs=(
            P(None, ("grp", "leaf")),
            P(None, ("grp", "leaf")),
            P(("grp", "leaf"), None),
            P(("grp", "leaf"), None, None),
            P(("grp", "leaf")),
            P(),
            P(("grp", "leaf"), None),
            P(("grp", "leaf"), None),
            P("grp", None),
        ),
        out_specs=(P(None, ("grp", "leaf")), P(None, ("grp", "leaf"))),
        check_vma=False,
    )
```

profile of v0, /device:TPU:10, one launch (start us, length us, event | category | flops | bytes accessed | tf_op | source)
XLA Modules:
  0.0 289.5 jit_solution(12969170760022450725)
XLA Ops:
  0.6 0.0 copy-start
  0.6 2.9 collective-permute-start.2
  3.5 1.9 collective-permute-start
  5.5 4.5 %collective-permute-start.3 = (f32[16,1024]{1,0:T(8,128)}, f32[16,1024]{1,0:T(8,128)S(1)}, u32[]{:S(2)}, u32[]{:S(2)}) collective-permute-start(f32[16,1024]{1,0:T(8,128)} %param.14), channel_id=1, source_target_pairs={{1,0},{2,1},{3,2},{4,3},{5,4},{6,5},{7,6},{8,7},{9,8},{10,9},{11,1... | collective-permute-start | bytes 196616 | tf_op jit(solution)/shard_map/ppermute | solution.py:17
  10.0 1.9 collective-permute-start.1
  12.0 1.0 copy.11
  12.9 0.7 fusion.35
  13.6 0.7 fusion.36
  14.2 1.3 fusion.39
  16.9 0.8 multiply_reduce_fusion.12
  17.7 1.2 fusion.41
  18.9 17.5 %all_gather.18 = f32[16,2048]{1,0:T(8,128)S(1)} all-gather(f32[16,128]{1,0:T(8,128)S(1)} %fusion.41), channel_id=1, replica_groups=mesh['grp'=2,'leaf'=16] {'leaf'}, dimensions={1}, use_global_device_ids=true | all-gather | bytes 139264 | tf_op jit(solution)/shard_map/all_gather | solution.py:85
  36.4 1.0 fusion.26
  37.4 25.1 %psum.43 = f32[16,128]{1,0:T(8,128)S(1)} all-reduce(f32[16,128]{1,0:T(8,128)S(1)} %fusion.26), channel_id=1, replica_groups=mesh['grp'=2,'leaf'=16] {'leaf'}, use_global_device_ids=true, to_apply=%region_13.14 | all-reduce | flops 2048 | bytes 16384 | tf_op jit(solution)/shard_map/psum | solution.py:86
  62.5 4.4 %all_gather.20 = f32[16,256]{1,0:T(8,128)S(1)} all-gather(f32[16,128]{1,0:T(8,128)S(1)} %psum.43), channel_id=1, replica_groups=mesh['grp'=2,'leaf'=16] {'grp'}, dimensions={1}, use_global_device_ids=true | all-gather | bytes 24576 | tf_op jit(solution)/shard_map/all_gather | solution.py:87
  66.8 0.6 gather_fusion
  67.5 25.8 %all-gather = f32[8,2048]{0,1:T(8,128)S(1)} all-gather(f32[8,128]{0,1:T(8,128)S(1)} %bitcast.71), channel_id=2, replica_groups=mesh['grp'=2,'leaf'=16] {'leaf'}, dimensions={1}, use_global_device_ids=true | all-gather | bytes 69632 | tf_op jit(solution)/shard_map/all_gather | solution.py:57
  93.2 1.0 multiply_reduce_fusion.4
  94.2 0.6 gather_fusion.1
  94.9 0.8 multiply_reduce_fusion.9
  95.7 5.0 %all-gather.1 = f32[8,256]{0,1:T(8,128)S(1)} all-gather(f32[8,128]{0,1:T(8,128)S(1)} %bitcast.70), channel_id=3, replica_groups=mesh['grp'=2,'leaf'=16] {'grp'}, dimensions={1}, use_global_device_ids=true | all-gather | bytes 12288 | tf_op jit(solution)/shard_map/all_gather | solution.py:59
  100.7 0.8 multiply_reduce_fusion.5
  101.5 0.0 copy-start.8
  101.5 6.9 %exponential_multiply_fusion.2 = f32[1024,1024]{1,0:T(8,128)S(1)} fusion(f32[1024]{0:T(1024)S(1)} %multiply_reduce_fusion.12, f32[8,1024]{1,0:T(8,128)} %param.13, f32[8]{0:T(128)} %param.18), kind=kOutput, calls=%fused_computation.14 | convolution fusion | flops 112205824 | bytes 4231200 | tf_op jit(solution)/shard_map/dot_general | solution.py:25
  108.3 0.0 copy-start.5
  108.4 0.0 copy-start.4
  108.4 1.6 exponential_multiply_fusion.3
  110.0 0.0 copy-start.6
  110.0 0.9 fusion.42
  110.9 0.4 exponential_multiply_fusion.4
  111.3 0.2 fusion.43
  111.5 0.0 copy-done.5
  111.5 0.2 convolution_add_fusion.3
  111.7 0.0 copy-done.4
  111.7 2.3 convolution_multiply_fusion.3
  114.1 0.0 copy-done.3
  114.1 0.5 fusion.44
  115.9 0.0 collective-permute-done
  115.9 2.5 conditional.2
  115.9 2.5 broadcast.88
  118.4 2.5 conditional.3
  118.4 2.5 broadcast.94
  120.9 4.6 %fusion.40 = f32[1024,16]{0,1:T(8,128)S(1)} fusion(f32[1024,1024]{1,0:T(8,128)} %get-tuple-element.49, f32[16,1024]{1,0:T(8,128)S(1)} %collective-permute-done.3), kind=kOutput, calls=%fused_computation.77 | convolution fusion | flops 201326592 | bytes 4325376 | tf_op jit(solution)/shard_map/dot_general | solution.py:42
  125.5 0.0 collective-permute-done.1
  125.6 2.4 multiply_reduce_fusion.8
  128.0 49.4 %all-reduce.1 = (f32[16]{0:T(128)S(1)}, f32[16]{0:T(128)S(1)}) all-reduce(f32[16]{0:T(128)S(1)} %get-tuple-element.33, f32[16]{0:T(128)S(1)} %get-tuple-element.32), channel_id=1, replica_groups=mesh['grp'=2,'leaf'=16] {'grp','leaf'}, use_global_device_ids=true, to_apply=%region_1.0 | all-reduce | flops 32 | bytes 256 | tf_op jit(solution)/shard_map/psum | solution.py:46
  177.4 0.1 multiply_subtract_fusion.1
  177.4 4.3 %convolution_multiply_fusion.2 = f32[16,1024]{1,0:T(8,128)S(1)} fusion(f32[16,1024]{1,0:T(8,128)S(1)} %multiply_subtract_fusion.1, f32[1024,1024]{1,0:T(8,128)} %copy-done.3, f32[]{:T(128)} %bitcast), kind=kOutput, calls=%fused_computation.26 | convolution fusion | flops 201342976 | bytes 4325380 | tf_op jit(solution)/shard_map/dot_general | solution.py:42
  181.7 0.4 fusion.46
  182.1 1.9 collective-permute-start.5
  184.0 2.4 collective-permute-start.4
  186.4 0.2 fusion.23
  186.6 16.7 %all_gather.22 = f32[16,2048]{1,0:T(8,128)S(1)} all-gather(f32[16,128]{1,0:T(8,128)S(1)} %fusion.46), channel_id=1, replica_groups=mesh['grp'=2,'leaf'=16] {'leaf'}, dimensions={1}, use_global_device_ids=true | all-gather | bytes 139264 | tf_op jit(solution)/shard_map/all_gather | solution.py:85
  203.3 25.0 %psum.46 = f32[16,128]{1,0:T(8,128)S(1)} all-reduce(f32[16,128]{1,0:T(8,128)S(1)} %fusion.23), channel_id=1, replica_groups=mesh['grp'=2,'leaf'=16] {'leaf'}, use_global_device_ids=true, to_apply=%region_20.0 | all-reduce | flops 2048 | bytes 16384 | tf_op jit(solution)/shard_map/psum | solution.py:86
  228.3 4.5 %all_gather.23 = f32[16,256]{1,0:T(8,128)S(1)} all-gather(f32[16,128]{1,0:T(8,128)S(1)} %psum.46), channel_id=1, replica_groups=mesh['grp'=2,'leaf'=16] {'grp'}, dimensions={1}, use_global_device_ids=true | all-gather | bytes 24576 | tf_op jit(solution)/shard_map/all_gather | solution.py:87
  232.8 0.2 fusion.48
  233.0 1.0 fusion.47
  234.0 0.2 convolution_add_fusion.2
  234.1 0.0 collective-permute-done.5
  234.2 4.3 %fusion.45 = f32[16,1024]{1,0:T(8,128)S(1)} fusion(f32[16,1024]{1,0:T(8,128)S(1)} %collective-permute-done.5, f32[1024,1024]{1,0:T(8,128)} %get-tuple-element.49), kind=kOutput, calls=%fused_computation.82 | convolution fusion | flops 201326592 | bytes 4325376 | tf_op jit(solution)/shard_map/dot_general | solution.py:42
  238.5 2.1 fusion.18
  240.6 0.6 multiply_reduce_fusion.6
  241.2 47.5 %all-reduce = (f32[16]{0:T(128)S(1)}, f32[16]{0:T(128)S(1)}) all-reduce(f32[16]{0:T(128)S(1)} %get-tuple-element.31, f32[16]{0:T(128)S(1)} %get-tuple-element.30), channel_id=1, replica_groups=mesh['grp'=2,'leaf'=16] {'grp','leaf'}, use_global_device_ids=true, to_apply=%region_19.0 | all-reduce | flops 32 | bytes 256 | tf_op jit(solution)/shard_map/psum | solution.py:46
  288.8 0.7 multiply_subtract_fusion
  (17 shorter events, 0.1 us)
Async XLA Ops:
  0.6 17.1 %copy-start = (f32[1024,128]{1,0:T(8,128)S(1)}, f32[1024,128]{1,0:T(8,128)}, u32[]{:S(2)}) copy-start(f32[1024,128]{1,0:T(8,128)} %param.15) | copy-start | bytes 1572868
  0.6 117.8 %collective-permute-start.2 = (f32[8,1024]{1,0:T(8,128)}, f32[8,1024]{1,0:T(8,128)S(1)}, u32[]{:S(2)}, u32[]{:S(2)}) collective-permute-start(f32[8,1024]{1,0:T(8,128)} %param.13), channel_id=1, source_target_pairs={{1,0},{2,1},{3,2},{4,3},{5,4},{6,5},{7,6},{8,7},{9,8},{10,9},{11,1... | collective-permute-start | bytes 98312 | tf_op jit(solution)/shard_map/ppermute | solution.py:17
  3.5 112.4 %collective-permute-start = (f32[8,1024]{1,0:T(8,128)}, f32[8,1024]{1,0:T(8,128)S(1)}, u32[]{:S(2)}, u32[]{:S(2)}) collective-permute-start(f32[8,1024]{1,0:T(8,128)} %param.13), channel_id=1, source_target_pairs={{0,1},{1,2},{2,3},{3,4},{4,5},{5,6},{6,7},{7,8},{8,9},{9,10},{10,1... | collective-permute-start | bytes 98312 | tf_op jit(solution)/shard_map/ppermute | solution.py:16
  5.5 115.5 %collective-permute-start.3 = (f32[16,1024]{1,0:T(8,128)}, f32[16,1024]{1,0:T(8,128)S(1)}, u32[]{:S(2)}, u32[]{:S(2)}) collective-permute-start(f32[16,1024]{1,0:T(8,128)} %param.14), channel_id=1, source_target_pairs={{1,0},{2,1},{3,2},{4,3},{5,4},{6,5},{7,6},{8,7},{9,8},{10,9},{11,1... | collective-permute-start | bytes 196616 | tf_op jit(solution)/shard_map/ppermute | solution.py:17
  10.0 115.5 %collective-permute-start.1 = (f32[16,1024]{1,0:T(8,128)}, f32[16,1024]{1,0:T(8,128)S(1)}, u32[]{:S(2)}, u32[]{:S(2)}) collective-permute-start(f32[16,1024]{1,0:T(8,128)} %param.14), channel_id=1, source_target_pairs={{0,1},{1,2},{2,3},{3,4},{4,5},{5,6},{6,7},{7,8},{8,9},{9,10},{10,1... | collective-permute-start | bytes 196616 | tf_op jit(solution)/shard_map/ppermute | solution.py:16
  101.5 6.9 %copy-start.8 = (f32[8]{0:T(128)S(1)}, f32[8]{0:T(128)}, u32[]{:S(2)}) copy-start(f32[8]{0:T(128)} %param.18) | copy-start | bytes 100
  108.3 5.7 %copy-start.3 = (f32[1024,1024]{1,0:T(8,128)}, f32[1024,1024]{1,0:T(8,128)S(1)}, u32[]{:S(2)}) copy-start(f32[1024,1024]{1,0:T(8,128)S(1)} %exponential_multiply_fusion.2) | copy-start | bytes 12582916
  108.3 3.1 %copy-start.5 = (f32[1,128,128]{2,1,0:T(8,128)S(1)}, f32[1,128,128]{2,1,0:T(8,128)}, u32[]{:S(2)}) copy-start(f32[1,128,128]{2,1,0:T(8,128)} %param.16) | copy-start | bytes 196612
  108.4 3.4 %copy-start.4 = (f32[16,1024]{1,0:T(8,128)S(1)}, f32[16,1024]{1,0:T(8,128)}, u32[]{:S(2)}) copy-start(f32[16,1024]{1,0:T(8,128)} %param.14) | copy-start | bytes 196612
  110.0 5.9 %copy-start.6 = (f32[8,1024]{1,0:T(8,128)S(1)}, f32[8,1024]{1,0:T(8,128)}, u32[]{:S(2)}) copy-start(f32[8,1024]{1,0:T(8,128)} %param.13) | copy-start | bytes 98308
  120.9 4.6 %copy-start.7 = (f32[1024]{0:T(1024)S(1)}, f32[1024]{0:T(1024)}, u32[]{:S(2)}) copy-start(f32[1024]{0:T(1024)} %param.17) | copy-start | bytes 12292
  120.9 4.6 %copy-start.1 = (f32[1024,1024]{1,0:T(8,128)S(1)}, f32[1024,1024]{1,0:T(8,128)}, u32[]{:S(2)}) copy-start(f32[1024,1024]{1,0:T(8,128)} %get-tuple-element.48) | copy-start | bytes 12582916
  182.1 52.1 %collective-permute-start.5 = (f32[16,1024]{1,0:T(8,128)S(1)}, f32[16,1024]{1,0:T(8,128)S(1)}, u32[]{:S(2)}, u32[]{:S(2)}) collective-permute-start(f32[16,1024]{1,0:T(8,128)S(1)} %multiply_subtract_fusion.1), channel_id=1, source_target_pairs={{1,0},{2,1},{3,2},{4,3},{5,4},{6,5},{7,6},{8,7},{9,8},{10,9},{11,1... | collective-permute-start | bytes 196616 | tf_op jit(solution)/shard_map/ppermute | solution.py:17
  184.0 54.5 %collective-permute-start.4 = (f32[16,1024]{1,0:T(8,128)S(1)}, f32[16,1024]{1,0:T(8,128)S(1)}, u32[]{:S(2)}, u32[]{:S(2)}) collective-permute-start(f32[16,1024]{1,0:T(8,128)S(1)} %multiply_subtract_fusion.1), channel_id=1, source_target_pairs={{0,1},{1,2},{2,3},{3,4},{4,5},{5,6},{6,7},{7,8},{8,9},{9,10},{10,1... | collective-permute-start | bytes 196616 | tf_op jit(solution)/shard_map/ppermute | solution.py:16
  228.3 10.2 %copy-start.2 = (f32[1024,1024]{1,0:T(8,128)S(1)}, f32[1024,1024]{1,0:T(8,128)}, u32[]{:S(2)}) copy-start(f32[1024,1024]{1,0:T(8,128)} %get-tuple-element.48) | copy-start | bytes 12582916
where the time goes:
time: 290 us
  blocking collectives  221 us (76%)
  matrix products  35.3 us (12%)
  starting transfers between devices  15.6 us (5%)
  local copies, waits for them, and re-layouts  8.64 us (3%)
  other arithmetic  5.55 us (2%)
  between operations  3.6 us (1%)
    psum x2, blocking collectives, two_products(): lax.psum((jnp.sum(residual * residual, axis=1), jnp.sum(residual * image,...  96.9 us
    psum x2, blocking collectives, apply(): group_coeff = lax.psum(product(coeff, lift), 'leaf')  50.1 us
    all_gather x2, blocking collectives, apply(): lax.all_gather(coeff, 'leaf', axis=1, tiled=True)  34.1 us
    all_gather x1, blocking collectives, local(): group_pts = lax.all_gather(skel_pts, 'leaf', axis=1, tiled=True)  25.8 us
    dot_general x10, matrix products, product(): return jnp.dot(first, second, precision=lax.Precision.HIGHEST)  22.7 us
    ppermute x3, starting transfers between devices, padded_2(): after = lax.ppermute(initial, axis, down)  9.35 us
    all_gather x2, blocking collectives, apply(): top_coeff = lax.all_gather(group_coeff, 'grp', axis=1, tiled=True)  8.85 us
    dot_general x3, matrix products, kernel_block(): lax.dot_general(first, second, (((0,), (0,)), ((), ())), precision=lax.Pr...  8.84 us
  transfers between devices with their start and end apart: 6, of which 0 were waited for; matrix products, arithmetic and copies ran while one was open for 13% of the time, Pallas kernels for 0%

commit v1 on v0

--- a/solution.py
+++ b/solution.py
@@ -54,7 +54,7 @@
     right_bit = links[0, 1]
     weight_self = 1.0 + (left_bit + right_bit).astype(jnp.float32)
     skel_pts = points[:, leaf_skel[0]]
-    group_pts = lax.all_gather(skel_pts, "leaf", axis=1, tiled=True)
+    group_pts = jnp.concatenate(lax.all_gather(skel_pts, "leaf"), axis=1)
     top_pts = group_pts[:, group_skel[0]]
     top_all = lax.all_gather(top_pts, "grp", axis=1, tiled=True)
     kernel_top = kernel_block(top_pts, top_all, inv_scale)

time: 290 us -> 288 us (level)
  blocking collectives: 221 us -> 218 us
    all_gather x1, blocking collectives: 25.8 us -> 22.6 us  [local(): group_pts = jnp.concatenate(lax.all_gather(skel_pts, 'leaf'), axis=1)]
  transfers between devices with their start and end apart: 6 -> 6, of which waited for: 0 -> 0; matrix products, arithmetic and copies ran while one was open for 13% -> 14% of each run, Pallas kernels for 0% -> 0%
where the time goes in v1:
time: 288 us; the launch traced here: 287 us
  blocking collectives  218 us (76%)
  matrix products  35.3 us (12%)
  starting transfers between devices  15.6 us (5%)
  local copies, waits for them, and re-layouts  9.02 us (3%)
  other arithmetic  5.3 us (2%)
  between operations  3.61 us (1%)
    psum x2, blocking collectives, two_products(): lax.psum((jnp.sum(residual * residual, axis=1), jnp.sum(residual * image,...  97.2 us
    psum x2, blocking collectives, apply(): group_coeff = lax.psum(product(coeff, lift), 'leaf')  50.1 us
    all_gather x2, blocking collectives, apply(): lax.all_gather(coeff, 'leaf', axis=1, tiled=True)  34 us
    dot_general x10, matrix products, product(): return jnp.dot(first, second, precision=lax.Precision.HIGHEST)  22.7 us
    all_gather x1, blocking collectives, local(): group_pts = jnp.concatenate(lax.all_gather(skel_pts, 'leaf'), axis=1)  22.6 us
    ppermute x3, starting transfers between devices, padded_2(): after = lax.ppermute(initial, axis, down)  9.35 us
    all_gather x2, blocking collectives, apply(): top_coeff = lax.all_gather(group_coeff, 'grp', axis=1, tiled=True)  8.85 us
    dot_general x3, matrix products, kernel_block(): lax.dot_general(first, second, (((0,), (0,)), ((), ())), precision=lax.Pr...  8.85 us
  transfers between devices with their start and end apart: 6, of which 0 were waited for; matrix products, arithmetic and copies ran while one was open for 14% of the time, Pallas kernels for 0%

profile of v1, /device:TPU:10, one launch (start us, length us, event | category | flops | bytes accessed | tf_op | source)
XLA Modules:
  0.0 286.6 jit_solution(1450332741347102196)
XLA Ops:
  0.6 0.0 copy-start
  0.6 2.9 %collective-permute-start.2 = (f32[8,1024]{1,0:T(8,128)}, f32[8,1024]{1,0:T(8,128)S(1)}, u32[]{:S(2)}, u32[]{:S(2)}) collective-permute-start(f32[8,1024]{1,0:T(8,128)} %param.13), channel_id=1, source_target_pairs={{1,0},{2,1},{3,2},{4,3},{5,4},{6,5},{7,6},{8,7},{9,8},{10,9},{11,1... | collective-permute-start | bytes 98312 | tf_op jit(solution)/shard_map/ppermute | solution.py:17
  3.5 1.9 collective-permute-start
  5.5 4.5 %collective-permute-start.3 = (f32[16,1024]{1,0:T(8,128)}, f32[16,1024]{1,0:T(8,128)S(1)}, u32[]{:S(2)}, u32[]{:S(2)}) collective-permute-start(f32[16,1024]{1,0:T(8,128)} %param.14), channel_id=1, source_target_pairs={{1,0},{2,1},{3,2},{4,3},{5,4},{6,5},{7,6},{8,7},{9,8},{10,9},{11,1... | collective-permute-start | bytes 196616 | tf_op jit(solution)/shard_map/ppermute | solution.py:17
  10.0 1.9 collective-permute-start.1
  12.0 1.0 copy.16
  12.9 0.7 fusion.35
  13.6 0.7 fusion.36
  14.2 1.3 fusion.39
  16.9 0.8 multiply_reduce_fusion.12
  17.7 1.2 fusion.41
  18.9 17.5 %all_gather.21 = f32[16,2048]{1,0:T(8,128)S(1)} all-gather(f32[16,128]{1,0:T(8,128)S(1)} %fusion.41), channel_id=1, replica_groups=mesh['grp'=2,'leaf'=16] {'leaf'}, dimensions={1}, use_global_device_ids=true | all-gather | bytes 139264 | tf_op jit(solution)/shard_map/all_gather | solution.py:85
  36.4 1.0 fusion.26
  37.4 25.1 %psum.43 = f32[16,128]{1,0:T(8,128)S(1)} all-reduce(f32[16,128]{1,0:T(8,128)S(1)} %fusion.26), channel_id=1, replica_groups=mesh['grp'=2,'leaf'=16] {'leaf'}, use_global_device_ids=true, to_apply=%region_13.14 | all-reduce | flops 2048 | bytes 16384 | tf_op jit(solution)/shard_map/psum | solution.py:86
  62.5 4.4 %all_gather.24 = f32[16,256]{1,0:T(8,128)S(1)} all-gather(f32[16,128]{1,0:T(8,128)S(1)} %psum.43), channel_id=1, replica_groups=mesh['grp'=2,'leaf'=16] {'grp'}, dimensions={1}, use_global_device_ids=true | all-gather | bytes 24576 | tf_op jit(solution)/shard_map/all_gather | solution.py:87
  66.8 0.6 gather_fusion
  67.5 22.6 %all-gather = f32[128,128]{1,0:T(8,128)S(1)} all-gather(f32[8,128]{1,0:T(8,128)S(1)} %copy.17), channel_id=2, replica_groups=mesh['grp'=2,'leaf'=16] {'leaf'}, dimensions={0}, use_global_device_ids=true | all-gather | bytes 69632 | tf_op jit(solution)/shard_map/all_gather | solution.py:57
  90.1 0.7 multiply_reduce_fusion.9
  90.8 0.3 copy.18
  91.2 0.6 gather_fusion.1
  91.8 0.8 multiply_reduce_fusion.8
  92.6 5.0 %all-gather.1 = f32[8,256]{0,1:T(8,128)S(1)} all-gather(f32[8,128]{0,1:T(8,128)S(1)} %bitcast.79), channel_id=3, replica_groups=mesh['grp'=2,'leaf'=16] {'grp'}, dimensions={1}, use_global_device_ids=true | all-gather | bytes 12288 | tf_op jit(solution)/shard_map/all_gather | solution.py:59
  97.6 0.8 multiply_reduce_fusion.4
  98.4 0.0 copy-start.8
  98.4 6.9 %exponential_multiply_fusion.2 = f32[1024,1024]{1,0:T(8,128)S(1)} fusion(f32[1024]{0:T(1024)S(1)} %multiply_reduce_fusion.12, f32[8,1024]{1,0:T(8,128)} %param.13, f32[8]{0:T(128)} %param.18), kind=kOutput, calls=%fused_computation.14 | convolution fusion | flops 112205824 | bytes 4231200 | tf_op jit(solution)/shard_map/dot_general | solution.py:25
  105.3 0.0 copy-start.5
  105.3 0.0 copy-start.4
  105.3 1.6 exponential_multiply_fusion.3
  106.9 0.0 copy-start.6
  106.9 0.9 fusion.42
  107.9 0.4 exponential_multiply_fusion.4
  108.2 0.2 fusion.43
  108.4 0.0 copy-done.5
  108.5 0.2 convolution_add_fusion.3
  108.6 0.0 copy-done.4
  108.7 2.3 convolution_multiply_fusion.3
  111.0 0.0 copy-done.3
  111.0 0.5 fusion.44
  112.9 2.5 conditional.2
  112.9 2.5 broadcast.92
  115.4 2.5 conditional.3
  115.4 2.5 broadcast.98
  117.9 4.6 %fusion.40 = f32[1024,16]{0,1:T(8,128)S(1)} fusion(f32[1024,1024]{1,0:T(8,128)} %get-tuple-element.49, f32[16,1024]{1,0:T(8,128)S(1)} %collective-permute-done.3), kind=kOutput, calls=%fused_computation.77 | convolution fusion | flops 201326592 | bytes 4325376 | tf_op jit(solution)/shard_map/dot_general | solution.py:42
  122.5 0.0 collective-permute-done.1
  122.5 2.4 multiply_reduce_fusion.7
  124.9 50.2 %all-reduce.1 = (f32[16]{0:T(128)S(1)}, f32[16]{0:T(128)S(1)}) all-reduce(f32[16]{0:T(128)S(1)} %get-tuple-element.33, f32[16]{0:T(128)S(1)} %get-tuple-element.32), channel_id=1, replica_groups=mesh['grp'=2,'leaf'=16] {'grp','leaf'}, use_global_device_ids=true, to_apply=%region_1.0 | all-reduce | flops 32 | bytes 256 | tf_op jit(solution)/shard_map/psum | solution.py:46
  175.1 0.1 multiply_subtract_fusion.1
  175.2 4.3 %convolution_multiply_fusion.2 = f32[16,1024]{1,0:T(8,128)S(1)} fusion(f32[16,1024]{1,0:T(8,128)S(1)} %multiply_subtract_fusion.1, f32[1024,1024]{1,0:T(8,128)} %copy-done.3, f32[]{:T(128)} %bitcast), kind=kOutput, calls=%fused_computation.26 | convolution fusion | flops 201342976 | bytes 4325380 | tf_op jit(solution)/shard_map/dot_general | solution.py:42
  179.5 0.4 fusion.46
  179.8 1.9 collective-permute-start.5
  181.8 2.4 collective-permute-start.4
  184.2 0.2 fusion.23
  184.3 16.6 %all_gather.26 = f32[16,2048]{1,0:T(8,128)S(1)} all-gather(f32[16,128]{1,0:T(8,128)S(1)} %fusion.46), channel_id=1, replica_groups=mesh['grp'=2,'leaf'=16] {'leaf'}, dimensions={1}, use_global_device_ids=true | all-gather | bytes 139264 | tf_op jit(solution)/shard_map/all_gather | solution.py:85
  200.9 25.0 %psum.46 = f32[16,128]{1,0:T(8,128)S(1)} all-reduce(f32[16,128]{1,0:T(8,128)S(1)} %fusion.23), channel_id=1, replica_groups=mesh['grp'=2,'leaf'=16] {'leaf'}, use_global_device_ids=true, to_apply=%region_20.0 | all-reduce | flops 2048 | bytes 16384 | tf_op jit(solution)/shard_map/psum | solution.py:86
  226.0 4.5 %all_gather.27 = f32[16,256]{1,0:T(8,128)S(1)} all-gather(f32[16,128]{1,0:T(8,128)S(1)} %psum.46), channel_id=1, replica_groups=mesh['grp'=2,'leaf'=16] {'grp'}, dimensions={1}, use_global_device_ids=true | all-gather | bytes 24576 | tf_op jit(solution)/shard_map/all_gather | solution.py:87
  230.5 0.2 fusion.48
  230.6 1.0 fusion.47
  231.6 0.2 convolution_add_fusion.2
  231.8 0.0 collective-permute-done.5
  231.9 4.3 %fusion.45 = f32[16,1024]{1,0:T(8,128)S(1)} fusion(f32[16,1024]{1,0:T(8,128)S(1)} %collective-permute-done.5, f32[1024,1024]{1,0:T(8,128)} %get-tuple-element.49), kind=kOutput, calls=%fused_computation.82 | convolution fusion | flops 201326592 | bytes 4325376 | tf_op jit(solution)/shard_map/dot_general | solution.py:42
  236.1 2.1 fusion.18
  238.2 0.6 multiply_reduce_fusion.5
  238.9 47.0 %all-reduce = (f32[16]{0:T(128)S(1)}, f32[16]{0:T(128)S(1)}) all-reduce(f32[16]{0:T(128)S(1)} %get-tuple-element.31, f32[16]{0:T(128)S(1)} %get-tuple-element.30), channel_id=1, replica_groups=mesh['grp'=2,'leaf'=16] {'grp','leaf'}, use_global_device_ids=true, to_apply=%region_19.0 | all-reduce | flops 32 | bytes 256 | tf_op jit(solution)/shard_map/psum | solution.py:46
  285.9 0.7 multiply_subtract_fusion
  (19 shorter events, 0.1 us)
Async XLA Ops:
  0.6 17.1 %copy-start = (f32[1024,128]{1,0:T(8,128)S(1)}, f32[1024,128]{1,0:T(8,128)}, u32[]{:S(2)}) copy-start(f32[1024,128]{1,0:T(8,128)} %param.15) | copy-start | bytes 1572868
  0.6 114.7 %collective-permute-start.2 = (f32[8,1024]{1,0:T(8,128)}, f32[8,1024]{1,0:T(8,128)S(1)}, u32[]{:S(2)}, u32[]{:S(2)}) collective-permute-start(f32[8,1024]{1,0:T(8,128)} %param.13), channel_id=1, source_target_pairs={{1,0},{2,1},{3,2},{4,3},{5,4},{6,5},{7,6},{8,7},{9,8},{10,9},{11,1... | collective-permute-start | bytes 98312 | tf_op jit(solution)/shard_map/ppermute | solution.py:17
  3.5 109.3 %collective-permute-start = (f32[8,1024]{1,0:T(8,128)}, f32[8,1024]{1,0:T(8,128)S(1)}, u32[]{:S(2)}, u32[]{:S(2)}) collective-permute-start(f32[8,1024]{1,0:T(8,128)} %param.13), channel_id=1, source_target_pairs={{0,1},{1,2},{2,3},{3,4},{4,5},{5,6},{6,7},{7,8},{8,9},{9,10},{10,1... | collective-permute-start | bytes 98312 | tf_op jit(solution)/shard_map/ppermute | solution.py:16
  5.5 112.4 %collective-permute-start.3 = (f32[16,1024]{1,0:T(8,128)}, f32[16,1024]{1,0:T(8,128)S(1)}, u32[]{:S(2)}, u32[]{:S(2)}) collective-permute-start(f32[16,1024]{1,0:T(8,128)} %param.14), channel_id=1, source_target_pairs={{1,0},{2,1},{3,2},{4,3},{5,4},{6,5},{7,6},{8,7},{9,8},{10,9},{11,1... | collective-permute-start | bytes 196616 | tf_op jit(solution)/shard_map/ppermute | solution.py:17
  10.0 112.4 %collective-permute-start.1 = (f32[16,1024]{1,0:T(8,128)}, f32[16,1024]{1,0:T(8,128)S(1)}, u32[]{:S(2)}, u32[]{:S(2)}) collective-permute-start(f32[16,1024]{1,0:T(8,128)} %param.14), channel_id=1, source_target_pairs={{0,1},{1,2},{2,3},{3,4},{4,5},{5,6},{6,7},{7,8},{8,9},{9,10},{10,1... | collective-permute-start | bytes 196616 | tf_op jit(solution)/shard_map/ppermute | solution.py:16
  98.4 6.9 %copy-start.8 = (f32[8]{0:T(128)S(1)}, f32[8]{0:T(128)}, u32[]{:S(2)}) copy-start(f32[8]{0:T(128)} %param.18) | copy-start | bytes 100
  105.3 5.7 %copy-start.3 = (f32[1024,1024]{1,0:T(8,128)}, f32[1024,1024]{1,0:T(8,128)S(1)}, u32[]{:S(2)}) copy-start(f32[1024,1024]{1,0:T(8,128)S(1)} %exponential_multiply_fusion.2) | copy-start | bytes 12582916
  105.3 3.1 %copy-start.5 = (f32[1,128,128]{2,1,0:T(8,128)S(1)}, f32[1,128,128]{2,1,0:T(8,128)}, u32[]{:S(2)}) copy-start(f32[1,128,128]{2,1,0:T(8,128)} %param.16) | copy-start | bytes 196612
  105.3 3.4 %copy-start.4 = (f32[16,1024]{1,0:T(8,128)S(1)}, f32[16,1024]{1,0:T(8,128)}, u32[]{:S(2)}) copy-start(f32[16,1024]{1,0:T(8,128)} %param.14) | copy-start | bytes 196612
  106.9 5.9 %copy-start.6 = (f32[8,1024]{1,0:T(8,128)S(1)}, f32[8,1024]{1,0:T(8,128)}, u32[]{:S(2)}) copy-start(f32[8,1024]{1,0:T(8,128)} %param.13) | copy-start | bytes 98308
  117.9 4.6 %copy-start.7 = (f32[1024]{0:T(1024)S(1)}, f32[1024]{0:T(1024)}, u32[]{:S(2)}) copy-start(f32[1024]{0:T(1024)} %param.17) | copy-start | bytes 12292
  117.9 4.6 %copy-start.1 = (f32[1024,1024]{1,0:T(8,128)S(1)}, f32[1024,1024]{1,0:T(8,128)}, u32[]{:S(2)}) copy-start(f32[1024,1024]{1,0:T(8,128)} %get-tuple-element.48) | copy-start | bytes 12582916
  179.8 52.0 %collective-permute-start.5 = (f32[16,1024]{1,0:T(8,128)S(1)}, f32[16,1024]{1,0:T(8,128)S(1)}, u32[]{:S(2)}, u32[]{:S(2)}) collective-permute-start(f32[16,1024]{1,0:T(8,128)S(1)} %multiply_subtract_fusion.1), channel_id=1, source_target_pairs={{1,0},{2,1},{3,2},{4,3},{5,4},{6,5},{7,6},{8,7},{9,8},{10,9},{11,1... | collective-permute-start | bytes 196616 | tf_op jit(solution)/shard_map/ppermute | solution.py:17
  181.8 54.4 %collective-permute-start.4 = (f32[16,1024]{1,0:T(8,128)S(1)}, f32[16,1024]{1,0:T(8,128)S(1)}, u32[]{:S(2)}, u32[]{:S(2)}) collective-permute-start(f32[16,1024]{1,0:T(8,128)S(1)} %multiply_subtract_fusion.1), channel_id=1, source_target_pairs={{0,1},{1,2},{2,3},{3,4},{4,5},{5,6},{6,7},{7,8},{8,9},{9,10},{10,1... | collective-permute-start | bytes 196616 | tf_op jit(solution)/shard_map/ppermute | solution.py:16
  226.0 10.2 %copy-start.2 = (f32[1024,1024]{1,0:T(8,128)S(1)}, f32[1024,1024]{1,0:T(8,128)}, u32[]{:S(2)}) copy-start(f32[1024,1024]{1,0:T(8,128)} %get-tuple-element.48) | copy-start | bytes 12582916
